TPU v7x, 256 devices: a whole 4x4x8 slice. The times are simulated.
256 devices in a mesh: vox: 128 (over x, z, y), sub: 2 (over core).
Axes of the slice: x: 4, y: 4, z: 8, core: 2. Of those that a mesh axis runs over, the one named last changes fastest.
Arguments:
- movie: bfloat16 [262144, 4096], P(('vox', 'sub')), may hold values from -120 to 120
- test_matrix: bfloat16 [4096, 256], replicated, may hold values from -0.09375 to 0.09375
Outputs:
- basis: float32 [262144, 256], P(('vox', 'sub'))
- r_factor: float32 [256, 256], replicated
- projected: float32 [256, 4096], P(None, ('vox', 'sub'))
All inputs are finite; a program needn't handle non-finite values.
Results may differ from a plain program's by a relative error of at most 0.00063.
Values sent between devices are 32-bit elements; how exact they have to be, the bound alone decides.
A program may use at most 128 MiB of HBM per device.

v0:
```python
import jax
import jax.numpy as jnp
from jax import lax
from jax.sharding import PartitionSpec as P


def square_sum(matrix):
    return jnp.dot(matrix.T, matrix, precision=lax.Precision.HIGHEST)


def local(movie, test_matrix):
    sketch = jnp.dot(movie, test_matrix, preferred_element_type=jnp.float32)
    devices_all = lax.axis_size(("vox", "sub"))
    sketch_b = sketch.astype(jnp.bfloat16)
    partial_sum = lax.dot_general(
        sketch_b, movie, (((0,), (0,)), ((), ())), preferred_element_type=jnp.float32
    )
    columns = movie.shape[1] // devices_all
    total = lax.psum(partial_sum, ("vox", "sub"))
    mine = lax.dynamic_slice_in_dim(total, lax.axis_index(("vox", "sub")) * columns, columns, 1)
    gram = lax.psum(square_sum(sketch), ("vox", "sub"))
    lower = jnp.linalg.cholesky(gram)
    width = sketch.shape[1]
    identity = jnp.eye(width, dtype=jnp.float32)
    inverse = lax.linalg.triangular_solve(lower, identity, left_side=True, lower=True)
    scale = jnp.sqrt(jnp.float32(sketch.shape[0] * devices_all))
    basis = jnp.dot(sketch, inverse.T, precision=lax.Precision.HIGHEST) * scale
    projected = jnp.dot(inverse, mine, precision=lax.Precision.HIGHEST)
    return (basis, lower.T / scale, projected)


def solution(mesh):
    placed = (P(("vox", "sub"), None), P())
    return jax.shard_map(
        local,
        mesh=mesh,
        in_specs=placed,
        out_specs=(P(("vox", "sub"), None), P(), P(None, ("vox", "sub"))),
        check_vma=False,
    )
```

profile of v0, /device:TPU:2, one launch (start us, length us, event | category | flops | bytes accessed | tf_op | source)
XLA Modules:
  0.0 380.6 jit_solution(14960276804258986143)
XLA Ops:
  7.2 0.0 copy-start
  7.2 0.0 all-reduce.4.cloned.1.call-start
  7.2 1.5 copy-done
  8.8 0.0 copy-start.1
  8.8 5.9 %fusion.17 = f32[1024,256]{1,0:T(8,128)S(1)} fusion(bf16[1024,4096]{1,0:T(8,128)(2,1)} %param.2, bf16[4096,256]{1,0:T(8,128)(2,1)S(1)} %copy-done), kind=kOutput, calls=%fused_computation.40 | convolution fusion | flops 2147483648 | bytes 11534336 | tf_op jit(solution)/shard_map/dot_general | solution.py:12
  14.6 0.0 copy-done.1
  14.6 4.3 %fusion = f32[256,4096]{1,0:T(8,128)} fusion(bf16[1024,4096]{1,0:T(8,128)(2,1)S(1)} %copy-done.1, f32[1024,256]{1,0:T(8,128)S(1)} %fusion.17), kind=kOutput, calls=%fused_computation.5 | convolution fusion | flops 2147745792 | bytes 13631488 | tf_op jit(solution)/shard_map/dot_general | solution.py:15
  19.0 2.5 fusion.18
  21.5 0.0 all-reduce.4.cloned.1.call-update
  21.6 0.6 iota_compare_fusion
  22.2 274.1 %all-reduce.4.cloned.1.call-done = (f32[256,256]{0,1:T(8,128)}, f32[256,4096]{1,0:T(8,128)}) async-done(((f32[256,256]{0,1:T(8,128)}, f32[256,4096]{1,0:T(8,128)}), (f32[256,256]{0,1:T(8,128)}, f32[256,4096]{1,0:T(8,128)})) %all-reduce.4.cloned.1.call-update) | async-done | bytes 4456464 | tf_op jit(solution)/shard_map/psum | solution.py:21
  296.3 1.1 copy.6
  297.3 1.0 fusion.2
  298.3 0.0 copy-start.3
  298.3 0.7 copy-done.3
  299.0 11.7 %cholesky.50 = f32[128,128]{1,0:T(8,128)S(1)} custom-call(f32[128,128]{1,0:T(8,128)S(1)} %cholesky.118), custom_call_target="Cholesky" | custom-call | tf_op jit(solution)/shard_map/jit(cholesky)/cholesky | solution.py:22
  310.8 9.8 %custom-call.14 = f32[1,128,128]{1,2,0:T(8,128)S(1)} custom-call(f32[1,128,128]{2,1,0:T(8,128)S(1)} %get-tuple-element.31), custom_call_target="InvertDiagBlocksLowerTriangular" | custom-call | tf_op jit(solution)/shard_map/jit(cholesky)/cholesky | solution.py:22
  320.6 0.2 cholesky.113
  320.8 1.0 constant_dynamic-update-slice_fusion
  321.9 1.1 convolution_subtract_fusion.1
  323.0 11.7 %cholesky.105 = f32[128,128]{1,0:T(8,128)S(1)} custom-call(f32[128,128]{1,0:T(8,128)S(1)} %convolution_subtract_fusion.1), custom_call_target="Cholesky" | custom-call | tf_op jit(solution)/shard_map/jit(cholesky)/cholesky | solution.py:22
  334.7 0.0 copy-start.2
  334.7 0.7 compare_reduce_fusion
  336.7 0.0 copy-done.2
  336.7 1.7 multiply_bitcast_fusion
  338.4 0.1 triangular_solve.63
  338.5 5.2 %while.1 = (s32[]{:T(128)}, f32[256,256]{1,0:T(8,128)S(1)}, s32[2,2]{1,0:T(2,128)S(1)}, f32[2,128,128]{2,1,0:T(8,128)}, s32[]{:T(128)}) while((s32[]{:T(128)}, f32[256,256]{1,0:T(8,128)S(1)}, s32[2,2]{1,0:T(2,128)S(1)}, f32[2,128,128]{2,1,0:T(8,128)}, s32[]{:T(128)}) %tuple.29), condition=%wide.while_cond, body=%wide.while_body.sunk | while | flops 2 | bytes 132705 | solution.py:25
  338.5 0.6 fusion.30
  339.1 2.0 bitcast_dynamic-update-slice_fusion.2
  341.1 0.6 fusion.30
  341.7 2.0 bitcast_dynamic-update-slice_fusion.2
  343.7 21.1 %custom-call.15 = f32[2,128,128]{1,2,0:T(8,128)} custom-call(f32[2,128,128]{2,1,0:T(8,128)} %get-tuple-element.10), custom_call_target="InvertDiagBlocksLowerTriangular" | custom-call | tf_op jit(solution)/shard_map/triangular_solve | solution.py:25
  364.8 1.1 fusion.6
  365.9 1.0 convolution_subtract_fusion
  366.9 1.2 fusion.9
  368.1 2.0 convolution_multiply_fusion
  370.1 1.8 copy.7
  371.8 1.9 fusion.4
  (7 shorter events, 0.1 us)
Async XLA Ops:
  7.2 1.6 copy-start
  7.2 289.1 %all-reduce.4.cloned.1.call-start = ((), (), s32[]{:S(2)}) async-start(), calls=%async_computation | async-start | bytes 8912896 | tf_op jit(solution)/shard_map/psum | solution.py:21
  8.8 5.9 %copy-start.1 = (bf16[1024,4096]{1,0:T(8,128)(2,1)S(1)}, bf16[1024,4096]{1,0:T(8,128)(2,1)}, u32[]{:S(2)}) copy-start(bf16[1024,4096]{1,0:T(8,128)(2,1)} %param.2) | copy-start | bytes 25165828
  298.3 0.7 copy-start.3
  334.7 2.0 copy-start.2
Sparse Core Ops, SparseCore 0:
  21.7 274.5 all-reduce.3
where the time goes:
time: 381 us
  waiting for transfers between devices  274 us (72%)
  other arithmetic  58.5 us (15%)
  matrix products  22.1 us (6%)
  between operations  15.4 us (4%)
  local copies, waits for them, and re-layouts  10.6 us (3%)
    psum x1, waiting for transfers between devices, local(): gram = lax.psum(square_sum(sketch), ('vox', 'sub'))  274 us
    another operation x6, other arithmetic, local(): lower = jnp.linalg.cholesky(gram)  34 us
    another operation x2, other arithmetic, local(): lax.linalg.triangular_solve(lower, identity, left_side=True, lower=True)  21.1 us
  transfers between devices with their start and end apart: 1, of which 1 were waited for; matrix products, arithmetic and copies ran while one was open for 0% of the time, Pallas kernels for 0%

commit v1 on v0

--- a/solution.py
+++ b/solution.py
@@ -18,7 +18,7 @@
     columns = movie.shape[1] // devices_all
     total = lax.psum(partial_sum, ("vox", "sub"))
     mine = lax.dynamic_slice_in_dim(total, lax.axis_index(("vox", "sub")) * columns, columns, 1)
-    gram = lax.psum(square_sum(sketch), ("vox", "sub"))
+    gram = lax.psum(lax.psum(square_sum(sketch), "sub"), "vox")
     lower = jnp.linalg.cholesky(gram)
     width = sketch.shape[1]
     identity = jnp.eye(width, dtype=jnp.float32)

time: 381 us -> 555 us (1.46)
  waiting for transfers between devices: 274 us -> 444 us
    psum x1 -> x3, waiting for transfers between devices: 274 us -> 444 us  [the longest x2 246 us: local(): gram = lax.psum(lax.psum(square_sum(sketch), 'sub'), 'vox')]
  transfers between devices with their start and end apart: 1 -> 3, of which waited for: 1 -> 3; matrix products, arithmetic and copies ran while one was open for 0% -> 15% of each run, Pallas kernels for 0% -> 0%
where the time goes in v1:
time: 555 us; the launch traced here: 554 us
  waiting for transfers between devices  444 us (80%)
  other arithmetic  58.5 us (11%)
  matrix products  25.3 us (5%)
  between operations  15.1 us (3%)
  local copies, waits for them, and re-layouts  10.2 us (2%)
    psum x2, waiting for transfers between devices, local(): gram = lax.psum(lax.psum(square_sum(sketch), 'sub'), 'vox')  246 us
    psum x1, waiting for transfers between devices, local(): total = lax.psum(partial_sum, ('vox', 'sub'))  199 us
    another operation x6, other arithmetic, local(): lower = jnp.linalg.cholesky(gram)  34.1 us
    another operation x2, other arithmetic, local(): lax.linalg.triangular_solve(lower, identity, left_side=True, lower=True)  21.1 us
  transfers between devices with their start and end apart: 3, of which 3 were waited for; matrix products, arithmetic and copies ran while one was open for 15% of the time, Pallas kernels for 0%

profile of v1, /device:TPU:2, one launch (start us, length us, event | category | flops | bytes accessed | tf_op | source)
XLA Modules:
  0.0 553.9 jit_solution(2074768162319565386)
XLA Ops:
  7.2 0.0 copy-start
  7.2 0.0 all-reduce.5.cloned.1.call-start
  7.2 1.5 copy-done
  8.8 5.7 %fusion.17 = f32[1024,256]{1,0:T(8,128)S(1)} fusion(bf16[1024,4096]{1,0:T(8,128)(2,1)} %param.2, bf16[4096,256]{1,0:T(8,128)(2,1)S(1)} %copy-done), kind=kOutput, calls=%fused_computation.40 | convolution fusion | flops 2147483648 | bytes 11534336 | tf_op jit(solution)/shard_map/dot_general | solution.py:12
  14.5 2.5 fusion.18
  17.0 0.0 all-reduce.5.cloned.1.call-update
  17.0 0.0 all-reduce.7.cloned.1.call-start
  17.1 32.1 %all-reduce.5.cloned.1.call-done = f32[256,256]{0,1:T(8,128)} async-done(((f32[256,256]{0,1:T(8,128)}), f32[256,256]{0,1:T(8,128)}) %all-reduce.5.cloned.1.call-update) | async-done | bytes 262160 | tf_op jit(solution)/shard_map/psum | solution.py:21
  49.2 0.0 all-reduce.7.cloned.1.call-update
  49.2 0.2 all-reduce.9.cloned.1.call-start
  49.4 7.7 %fusion = f32[256,4096]{1,0:T(8,128)} fusion(bf16[1024,4096]{1,0:T(8,128)(2,1)} %param.2, f32[1024,256]{1,0:T(8,128)S(1)} %fusion.17), kind=kOutput, calls=%fused_computation.5 | convolution fusion | flops 2147745792 | bytes 13631488 | tf_op jit(solution)/shard_map/dot_general | solution.py:15
  57.2 0.0 all-reduce.9.cloned.1.call-update
  57.2 0.6 iota_compare_fusion
  57.9 213.8 %all-reduce.7.cloned.1.call-done = f32[256,256]{0,1:T(8,128)} async-done(((f32[256,256]{0,1:T(8,128)}), f32[256,256]{0,1:T(8,128)}) %all-reduce.7.cloned.1.call-update) | async-done | bytes 262160 | tf_op jit(solution)/shard_map/psum | solution.py:21
  271.6 1.1 copy.6
  272.7 1.0 fusion.2
  273.7 0.0 copy-start.2
  273.7 0.7 copy-done.2
  274.4 11.7 %cholesky.50 = f32[128,128]{1,0:T(8,128)S(1)} custom-call(f32[128,128]{1,0:T(8,128)S(1)} %cholesky.118), custom_call_target="Cholesky" | custom-call | tf_op jit(solution)/shard_map/jit(cholesky)/cholesky | solution.py:22
  286.2 9.8 %custom-call.14 = f32[1,128,128]{1,2,0:T(8,128)S(1)} custom-call(f32[1,128,128]{2,1,0:T(8,128)S(1)} %get-tuple-element.29), custom_call_target="InvertDiagBlocksLowerTriangular" | custom-call | tf_op jit(solution)/shard_map/jit(cholesky)/cholesky | solution.py:22
  296.0 1.0 constant_dynamic-update-slice_fusion
  297.0 1.1 convolution_subtract_fusion.1
  298.2 11.9 %cholesky.105 = f32[128,128]{1,0:T(8,128)S(1)} custom-call(f32[128,128]{1,0:T(8,128)S(1)} %convolution_subtract_fusion.1), custom_call_target="Cholesky" | custom-call | tf_op jit(solution)/shard_map/jit(cholesky)/cholesky | solution.py:22
  310.0 0.0 copy-start.1
  310.1 0.6 compare_reduce_fusion
  311.9 0.0 copy-done.1
  311.9 1.7 multiply_bitcast_fusion
  313.6 0.1 triangular_solve.63
  313.7 5.0 while.1
  313.7 0.6 fusion.30
  314.3 1.9 bitcast_dynamic-update-slice_fusion.2
  316.2 0.6 fusion.30
  316.8 1.9 bitcast_dynamic-update-slice_fusion.2
  318.7 21.1 %custom-call.15 = f32[2,128,128]{1,2,0:T(8,128)} custom-call(f32[2,128,128]{2,1,0:T(8,128)} %get-tuple-element.10), custom_call_target="InvertDiagBlocksLowerTriangular" | custom-call | tf_op jit(solution)/shard_map/triangular_solve | solution.py:25
  339.8 1.8 copy.7
  341.6 1.1 fusion.6
  342.7 1.0 convolution_subtract_fusion
  343.7 1.2 fusion.9
  344.9 2.0 convolution_multiply_fusion
  346.9 198.5 %all-reduce.9.cloned.1.call-done = f32[256,4096]{1,0:T(8,128)} async-done(((f32[256,4096]{1,0:T(8,128)}), f32[256,4096]{1,0:T(8,128)}) %all-reduce.9.cloned.1.call-update) | async-done | bytes 4194320 | tf_op jit(solution)/shard_map/psum | solution.py:19
  545.5 1.9 fusion.4
  (8 shorter events, 0.1 us)
Async XLA Ops:
  7.2 1.6 copy-start
  7.2 42.0 %all-reduce.5.cloned.1.call-start = ((), (), s32[]{:S(2)}) async-start(), calls=%async_computation | async-start | bytes 524288 | tf_op jit(solution)/shard_map/psum | solution.py:21
  17.0 254.6 %all-reduce.7.cloned.1.call-start = ((), (), s32[]{:S(2)}) async-start(), calls=%async_computation.1 | async-start | bytes 524288 | tf_op jit(solution)/shard_map/psum | solution.py:21
  49.2 496.2 %all-reduce.9.cloned.1.call-start = ((), (), s32[]{:S(2)}) async-start(), calls=%async_computation.2 | async-start | bytes 8388608 | tf_op jit(solution)/shard_map/psum | solution.py:19
  273.7 0.7 copy-start.2
  310.0 1.9 copy-start.1
Sparse Core Ops, SparseCore 0:
  17.1 31.9 all-reduce.4
  54.6 216.9 all-reduce.6
  277.1 268.3 all-reduce.8

commit v2 on v0

--- a/solution.py
+++ b/solution.py
@@ -18,7 +18,7 @@
     columns = movie.shape[1] // devices_all
     total = lax.psum(partial_sum, ("vox", "sub"))
     mine = lax.dynamic_slice_in_dim(total, lax.axis_index(("vox", "sub")) * columns, columns, 1)
-    gram = lax.psum(square_sum(sketch), ("vox", "sub"))
+    gram = jnp.sum(lax.all_gather(square_sum(sketch), ("vox", "sub")), axis=0)
     lower = jnp.linalg.cholesky(gram)
     width = sketch.shape[1]
     identity = jnp.eye(width, dtype=jnp.float32)

time: 381 us -> 515 us (1.35)
  waiting for transfers between devices: 274 us -> 383 us
  other arithmetic: 58.5 us -> 80.1 us
    all_gather x0 -> x1, waiting for transfers between devices: none -> 207 us  [local(): gram = jnp.sum(lax.all_gather(square_sum(sketch), ('vox', 'sub')), axis=0)]
    psum x1, waiting for transfers between devices: 274 us -> 176 us  [local(): total = lax.psum(partial_sum, ('vox', 'sub'))]
    reduce_sum x0 -> x1, other arithmetic: none -> 21.6 us  [local(): gram = jnp.sum(lax.all_gather(square_sum(sketch), ('vox', 'sub')), axis=0)]
  transfers between devices with their start and end apart: 1 -> 2, of which waited for: 1 -> 2; matrix products, arithmetic and copies ran while one was open for 0% -> 20% of each run, Pallas kernels for 0% -> 0%
where the time goes in v2:
time: 515 us; the launch traced here: 514 us
  waiting for transfers between devices  383 us (74%)
  other arithmetic  80.1 us (16%)
  matrix products  25.3 us (5%)
  between operations  15.5 us (3%)
  local copies, waits for them, and re-layouts  10.3 us (2%)
    all_gather x1, waiting for transfers between devices, local(): gram = jnp.sum(lax.all_gather(square_sum(sketch), ('vox', 'sub')), axis=0)  207 us
    psum x1, waiting for transfers between devices, local(): total = lax.psum(partial_sum, ('vox', 'sub'))  176 us
    another operation x6, other arithmetic, local(): lower = jnp.linalg.cholesky(gram)  34 us
    reduce_sum x1, other arithmetic, local(): gram = jnp.sum(lax.all_gather(square_sum(sketch), ('vox', 'sub')), axis=0)  21.6 us
    another operation x2, other arithmetic, local(): lax.linalg.triangular_solve(lower, identity, left_side=True, lower=True)  21.1 us
  transfers between devices with their start and end apart: 2, of which 2 were waited for; matrix products, arithmetic and copies ran while one was open for 20% of the time, Pallas kernels for 0%

profile of v2, /device:TPU:2, one launch (start us, length us, event | category | flops | bytes accessed | tf_op | source)
XLA Modules:
  0.0 514.2 jit_solution(8533228719686255634)
XLA Ops:
  7.2 0.0 copy-start
  7.2 0.0 all-gather.3.cloned.1.call-start
  7.2 1.5 copy-done
  8.8 5.7 %fusion.17 = f32[1024,256]{1,0:T(8,128)S(1)} fusion(bf16[1024,4096]{1,0:T(8,128)(2,1)} %param.2, bf16[4096,256]{1,0:T(8,128)(2,1)S(1)} %copy-done), kind=kOutput, calls=%fused_computation.40 | convolution fusion | flops 2147483648 | bytes 11534336 | tf_op jit(solution)/shard_map/dot_general | solution.py:12
  14.5 2.5 fusion.18
  17.0 0.0 all-gather.3.cloned.1.call-update
  17.0 0.0 all-reduce.3.cloned.1.call-start
  17.1 7.7 %fusion = f32[256,4096]{1,0:T(8,128)} fusion(bf16[1024,4096]{1,0:T(8,128)(2,1)} %param.2, f32[1024,256]{1,0:T(8,128)S(1)} %fusion.17), kind=kOutput, calls=%fused_computation.5 | convolution fusion | flops 2147745792 | bytes 13631488 | tf_op jit(solution)/shard_map/dot_general | solution.py:15
  24.8 0.0 all-reduce.3.cloned.1.call-update
  24.8 0.6 iota_compare_fusion
  25.5 206.6 %all-gather.3.cloned.1.call-done = f32[65536,256]{1,0:T(8,128)} async-done(((f32[256,256]{1,0:T(8,128)}), f32[65536,256]{1,0:T(8,128)}) %all-gather.3.cloned.1.call-update) | async-done | bytes 67108880 | tf_op jit(solution)/shard_map/all_gather | solution.py:21
  232.1 21.6 %reduce_sum.9 = f32[256,256]{1,0:T(8,128)S(1)} reduce(f32[256,256,256]{2,1,0:T(8,128)} %bitcast, f32[]{:T(128)} %constant.85.clone.1), dimensions={0}, to_apply=%region_0.0 | reduce | flops 16711680 | bytes 67371008 | tf_op jit(solution)/shard_map/reduce_sum | solution.py:21
  253.7 0.8 copy.7
  254.6 1.0 fusion.2
  255.6 0.0 copy-start.2
  255.6 0.7 copy-done.2
  256.3 11.7 %cholesky.50 = f32[128,128]{1,0:T(8,128)S(1)} custom-call(f32[128,128]{1,0:T(8,128)S(1)} %cholesky.118), custom_call_target="Cholesky" | custom-call | tf_op jit(solution)/shard_map/jit(cholesky)/cholesky | solution.py:22
  268.1 9.8 %custom-call.14 = f32[1,128,128]{1,2,0:T(8,128)S(1)} custom-call(f32[1,128,128]{2,1,0:T(8,128)S(1)} %get-tuple-element.32), custom_call_target="InvertDiagBlocksLowerTriangular" | custom-call | tf_op jit(solution)/shard_map/jit(cholesky)/cholesky | solution.py:22
  277.9 1.0 constant_dynamic-update-slice_fusion
  278.9 1.1 convolution_subtract_fusion.1
  280.0 11.7 %cholesky.105 = f32[128,128]{1,0:T(8,128)S(1)} custom-call(f32[128,128]{1,0:T(8,128)S(1)} %convolution_subtract_fusion.1), custom_call_target="Cholesky" | custom-call | tf_op jit(solution)/shard_map/jit(cholesky)/cholesky | solution.py:22
  291.8 0.0 copy-start.1
  291.8 0.7 compare_reduce_fusion
  293.9 0.0 copy-done.1
  293.9 1.7 multiply_bitcast_fusion
  295.6 0.1 triangular_solve.63
  295.6 5.3 %while.1 = (s32[]{:T(128)}, f32[256,256]{1,0:T(8,128)S(1)}, s32[2,2]{1,0:T(2,128)S(1)}, f32[2,128,128]{2,1,0:T(8,128)}, s32[]{:T(128)}) while((s32[]{:T(128)}, f32[256,256]{1,0:T(8,128)S(1)}, s32[2,2]{1,0:T(2,128)S(1)}, f32[2,128,128]{2,1,0:T(8,128)}, s32[]{:T(128)}) %tuple.30), condition=%wide.while_cond, body=%wide.while_body.sunk | while | flops 2 | bytes 132705 | solution.py:25
  295.6 0.6 fusion.30
  296.2 2.0 bitcast_dynamic-update-slice_fusion.2
  298.3 0.6 fusion.30
  298.9 2.0 bitcast_dynamic-update-slice_fusion.2
  300.9 21.1 %custom-call.15 = f32[2,128,128]{1,2,0:T(8,128)} custom-call(f32[2,128,128]{2,1,0:T(8,128)} %get-tuple-element.10), custom_call_target="InvertDiagBlocksLowerTriangular" | custom-call | tf_op jit(solution)/shard_map/triangular_solve | solution.py:25
  322.0 1.8 copy.8
  323.8 1.1 fusion.6
  324.9 1.0 convolution_subtract_fusion
  325.9 1.1 fusion.9
  327.1 2.0 convolution_multiply_fusion
  329.1 176.3 %all-reduce.3.cloned.1.call-done = f32[256,4096]{1,0:T(8,128)} async-done(((f32[256,4096]{1,0:T(8,128)}), f32[256,4096]{1,0:T(8,128)}) %all-reduce.3.cloned.1.call-update) | async-done | bytes 4194320 | tf_op jit(solution)/shard_map/psum | solution.py:19
  505.4 1.9 fusion.4
  (8 shorter events, 0.1 us)
Async XLA Ops:
  7.2 1.6 copy-start
  7.2 224.9 %all-gather.3.cloned.1.call-start = ((), (), s32[]{:S(2)}) async-start(), calls=%async_computation.1 | async-start | bytes 67371008 | tf_op jit(solution)/shard_map/all_gather | solution.py:21
  17.0 488.3 %all-reduce.3.cloned.1.call-start = ((), (), s32[]{:S(2)}) async-start(), calls=%async_computation | async-start | bytes 8388608 | tf_op jit(solution)/shard_map/psum | solution.py:19
  255.6 0.7 copy-start.2
  291.8 2.1 copy-start.1
Sparse Core Ops, SparseCore 0:
  17.2 214.8 all-gather.2
  237.6 267.7 all-reduce.2
